TPU v7x, 32 devices: a whole 2x2x4 slice. The times are simulated.
32 devices in a mesh: shot: 8 (over z, y), rcv: 4 (over x, core).
Axes of the slice: x: 2, y: 2, z: 4, core: 2. Of those that a mesh axis runs over, the one named last changes fastest.
Arguments:
- shot_data: bfloat16 [256, 1024, 256], P('shot', 'rcv'), may hold values from -0.375 to 0.375
- code: int32 [32, 256], P(None, 'shot'), may hold values from -1 to 1, as said below
- observed: bfloat16 [32, 1024, 256], P('shot', 'rcv'), may hold values from -6 to 6
- block_of: int32 [1024, 1], replicated, may hold values from 0 to 3; in each aligned block of 256 rows (0 to 255, 256 to 511, ...) at most 64 rows name the same one
- stencil_index: int32 [1024, 4], replicated, may hold values from 0 to 255
- stencil_weight: float32 [1024, 4], replicated, may hold values from -0.5 to 1
Outputs:
- adjoint_source: float32 [32, 1024, 256], P('shot', 'rcv')
Inputs may be any that keep to these rules, and one draw needn't show every extreme that they name: `code`: every entry is -1 or 1. `block_of`: among the receivers of one index of rcv (aligned blocks of 256 rows) at most 64 map to one model block.
All inputs are finite; a program needn't handle non-finite values.
Results may differ from a plain program's by a relative error of at most 0.0038.
Values may be sent and summed in bfloat16 or wider, within the bound.
A program may use at most 64 MiB of HBM per device.

v0:
```python
import functools

import jax
import jax.numpy as jnp
from jax import lax
from jax.experimental import pallas as pl
from jax.experimental.pallas import tpu as pltpu
from jax.sharding import PartitionSpec as P

GRID = 256
CAP = 64
ROWS = 16
LANES = 128
CUTS = 2
AHEAD = 2
LAG = 2.5
LOW_FIRST = (1, 4, 7, 10)
DIRECT = 2

BF16, F32 = jnp.bfloat16, jnp.float32
MESH = pl.DeviceIdType.MESH


def stages_of(piece, pieces, bits):
    rest = [(bit,) for bit in range(2, bits)]
    if bits == 1:
        return [(0,)]
    if piece >= pieces - DIRECT:
        return [(0,), tuple(range(1, bits))]
    if piece in LOW_FIRST:
        return [(1,), (0,)] + rest
    return [(0,), (1,)] + rest


def plan(pieces, bits):
    table, sems = [], 0
    for piece in range(pieces):
        left, slot, stages = list(range(1 << bits)), 0, []
        for group in stages_of(piece, pieces, bits):
            mask = sum(1 << bit for bit in group)
            kept = [m for m in left if not m & mask]
            peers = []
            for peer in range(1, 1 << bits):
                if peer & ~mask:
                    continue
                peers.append((peer, slot, sems))
                slot, sems = slot + len(kept), sems + 1
            stages.append((kept, peers))
            left = kept
        table.append(stages)
    return table, sems


def schedule(table, halves_of):
    tasks = []
    for p, stages in enumerate(table):
        tasks.append((max(p - AHEAD, -1), 0, p, "encode", 0))
        for s in range(len(stages) - 1):
            tasks.append((p + LAG * s, 1, p, "sum", s))
    for c, members in enumerate(halves_of):
        done = max(p + LAG * (len(table[p]) - 1) for p in members)
        tasks.append((done, 2, c, "finish", 0))
        tasks.append((done + LAG, 3, c, "inject", 0))
    return sorted(tasks)


def kernel(dims, table, shot_hbm, code_hbm, obs_hbm, blk_hbm, idx_hbm, wgt_hbm, out_hbm,
           out, shot, code_ref, obs, blk_ref, idx_ref, wgt_ref, signs, weights, acc, send, recv,
           send3, recv3, select, slotm, load_sem, ssem, rsem, s3, r3, out_sem):
    n, groups, owned, halves = dims
    bits = n.bit_length() - 1
    shots, rcv, _ = shot_hbm.shape
    part = rcv // CUTS
    chunks = owned * halves
    slots = groups * CAP
    me = lax.axis_index("shot")
    mine = lax.axis_index("rcv")

    def partner(mask):
        at = me
        for bit in range(bits):
            if mask >> bit & 1:
                own = lax.rem(lax.div(me, 1 << bit), 2)
                at = at + (1 << bit) - own * (2 << bit)
        return at

    partners = [partner(mask) for mask in range(n)]

    def rcv_peer(e):
        return lax.rem(mine + e, groups)

    def cut(h):
        return pl.ds(h * LANES, LANES)

    small = [(code_hbm, code_ref), (blk_hbm, blk_ref), (idx_hbm, idx_ref), (wgt_hbm, wgt_ref),
             (obs_hbm, obs)]
    small = [pltpu.make_async_copy(src, dst, load_sem.at[i]) for i, (src, dst) in enumerate(small)]
    loads = {}
    for h in range(halves):
        for q in range(CUTS):
            some = pl.ds(q * part, part)
            loads[h, q] = pltpu.make_async_copy(
                shot_hbm.at[:, some, cut(h)], shot.at[h, :, some, :],
                load_sem.at[len(small) + h * CUTS + q])
    small[0].start()
    for load in loads.values():
        load.start()
    for load in small[1:]:
        load.start()

    barrier = pltpu.get_barrier_semaphore()
    for mask in range(1, n):
        pl.semaphore_signal(barrier, inc=1, device_id={"shot": partners[mask]}, device_id_type=MESH)
    for e in range(1, groups):
        pl.semaphore_signal(barrier, inc=1, device_id={"rcv": rcv_peer(e)}, device_id_type=MESH)

    out_rows, depth = n * ROWS, shots * ROWS
    spread_s = (lax.broadcasted_iota(jnp.int32, (shots, depth), 1)
                - ROWS * lax.broadcasted_iota(jnp.int32, (shots, depth), 0))
    spread_s = ((spread_s >= 0) & (spread_s < ROWS)).astype(F32).astype(BF16)

    def widen(j):
        same_row = ((lax.broadcasted_iota(jnp.int32, (out_rows, depth), 0) & (ROWS - 1))
                    == (lax.broadcasted_iota(jnp.int32, (out_rows, depth), 1) & (ROWS - 1)))
        for m in range(n):
            line = code_ref[pl.ds(partners[m] * owned + j, 1), :].astype(F32)
            signs[j, m * ROWS:(m + 1) * ROWS, :] = jnp.broadcast_to(line, (ROWS, shots)).astype(BF16)
        wide = jnp.dot(signs[j], spread_s, preferred_element_type=F32)
        weights[j] = jnp.where(same_row, wide, 0.0).astype(BF16)

    def copies(p, s):
        kept, peers = table[p][s]
        return [pltpu.make_async_remote_copy(
            src_ref=send.at[p, pl.ds(slot, len(kept))], dst_ref=recv.at[p, pl.ds(slot, len(kept))],
            send_sem=ssem.at[sem], recv_sem=rsem.at[sem],
            device_id={"shot": partners[peer]}, device_id_type=MESH)
            for peer, slot, sem in peers]

    def copy3(c, e):
        return pltpu.make_async_remote_copy(
            src_ref=send3.at[c, e - 1], dst_ref=recv3.at[c, e], send_sem=s3.at[c, e - 1],
            recv_sem=r3.at[c, e - 1], device_id={"rcv": rcv_peer(e)}, device_id_type=MESH)

    def place(p):
        return p // (halves * CUTS), p // CUTS % halves, p % CUTS

    def encode(p, _):
        j, h, q = place(p)
        if h == 0 and q == 0:
            if j == 0:
                small[0].wait()
            widen(j)
        if j == 0:
            loads[h, q].wait()
        kept, peers = table[p][0]

        def tile(g, carry):
            rows = pl.ds(pl.multiple_of(g * ROWS, ROWS), ROWS)
            x = shot[h, :, pl.ds(pl.multiple_of(q * part + g * ROWS, ROWS), ROWS), :]
            y = jnp.dot(weights[j], x.reshape(depth, LANES), preferred_element_type=F32)
            y = y.reshape(n, ROWS, LANES)
            for m in kept:
                acc[p, m, rows, :] = y[m]
            for peer, slot, _ in peers:
                for i, m in enumerate(kept):
                    send[p, slot + i, rows, :] = y[m | peer].astype(BF16)
            return carry

        lax.fori_loop(0, part // ROWS, tile, 0, unroll=4)
        if p == 0:
            pl.semaphore_wait(barrier, n + groups - 2)
        for copy in copies(p, 0):
            copy.start()

    def received(p, s, m):
        kept, peers = table[p][s]
        total = acc[p, m]
        for _, slot, _ in peers:
            total = total + recv[p, slot + kept.index(m)].astype(F32)
        return total

    def sum_up(p, s):
        for copy in copies(p, s):
            copy.wait_recv()
        kept, peers = table[p][s + 1]
        for (peer, slot, _), copy in zip(peers, copies(p, s + 1)):
            for i, m in enumerate(kept):
                send[p, slot + i] = received(p, s, m | peer).astype(BF16)
            copy.start()
        for m in kept:
            acc[p, m] = received(p, s, m)

    def finish(c, _):
        j, h = c // halves, c % halves
        picked = jnp.zeros((slots, LANES), F32)
        for q in range(CUTS):
            p = c * CUTS + q
            for copy in copies(p, len(table[p]) - 1):
                copy.wait_recv()
            some = pl.ds(q * part, part)
            residual = received(p, len(table[p]) - 1, 0) - obs[j, some, cut(h)].astype(F32)
            picked = picked + jnp.dot(
                select[:, some], residual.astype(BF16), preferred_element_type=F32)
        picked = picked.astype(BF16)
        for e in range(1, groups):
            send3[c, e - 1] = picked[e * CAP:(e + 1) * CAP]
            copy3(c, e).start()
        recv3[c, 0] = picked[:CAP]

    def result(c):
        j, h = c // halves, c % halves
        return pltpu.make_async_copy(out.at[c], out_hbm.at[j, :, cut(h)], out_sem.at[c])

    def inject(c, _):
        for e in range(1, groups):
            copy3(c, e).wait_recv()
        arrived = recv3[c].reshape(slots, LANES)
        out[c] = jnp.dot(slotm[...], arrived, preferred_element_type=F32)
        result(c).start()

    def prepare():
        before = (lax.broadcasted_iota(jnp.int32, (rcv, rcv), 0)
                  < lax.broadcasted_iota(jnp.int32, (rcv, rcv), 1)).astype(F32).astype(BF16)
        slot_at = lax.broadcasted_iota(jnp.int32, (slots, rcv), 0)
        point_at = lax.broadcasted_iota(jnp.int32, (GRID, rcv), 0)
        block_at = lax.broadcasted_iota(jnp.int32, (max(16, groups), rcv), 0)

        def rank_of(ids):
            hot = (block_at == ids).astype(F32)
            count = jnp.dot(hot.astype(BF16), before, preferred_element_type=F32)
            return jnp.sum(hot * count, axis=0, keepdims=True).astype(jnp.int32)

        total = jnp.zeros((GRID, slots), F32)
        for e in range(groups):
            source = lax.rem(mine - e + groups, groups)
            at = pl.ds(pl.multiple_of(source * rcv, rcv), rcv)
            ids = blk_ref[:, at]
            rank = rank_of(ids)
            if e == 0:
                ahead = ids - mine
                ahead = jnp.where(ahead < 0, ahead + groups, ahead)
                select[...] = (slot_at == ahead * CAP + rank).astype(F32).astype(BF16)
            spread = jnp.zeros((GRID, rcv), F32)
            for w in range(idx_ref.shape[0]):
                spread = spread + jnp.where(
                    point_at == idx_ref[pl.ds(w, 1), at], wgt_ref[pl.ds(w, 1), at], 0.0)
            key = jnp.where(ids == mine, e * CAP + rank, -1)
            pick = (slot_at == key).astype(F32).astype(BF16)
            total = total + lax.dot_general(
                spread.astype(BF16), pick, (((1,), (1,)), ((), ())), preferred_element_type=F32)
        slotm[...] = total.astype(BF16)

    act = {"encode": encode, "sum": sum_up, "finish": finish, "inject": inject}
    prepared = False
    members = [[c * CUTS + q for q in range(CUTS)] for c in range(chunks)]
    for _, _, item, what, s in schedule(table, members):
        if what != "encode" and not prepared:
            for load in small[1:]:
                load.wait()
            prepare()
            prepared = True
        act[what](item, s)
    for p in range(len(table)):
        for s in range(len(table[p])):
            for copy in copies(p, s):
                copy.wait_send()
    for c in range(chunks):
        for e in range(1, groups):
            copy3(c, e).wait_send()
        result(c).wait()


def on_device(n_shot, n_rcv, shot_data, code, observed, block_of, stencil_index, stencil_weight):
    shots, rcv, samples = shot_data.shape
    owned = observed.shape[0]
    halves = samples // LANES
    chunks = owned * halves
    pieces = chunks * CUTS
    part = rcv // CUTS
    slots = n_rcv * CAP
    table, sems = plan(pieces, n_shot.bit_length() - 1)
    hbm = pl.BlockSpec(memory_space=pltpu.HBM)
    vmem = pltpu.VMEM
    dma = pltpu.SemaphoreType.DMA
    rows = (block_of.T, stencil_index.T, stencil_weight.T)
    return pl.pallas_call(
        functools.partial(kernel, (n_shot, n_rcv, owned, halves), table),
        out_shape=jax.ShapeDtypeStruct((owned, GRID, samples), F32),
        in_specs=[hbm] * 6,
        out_specs=hbm,
        scratch_shapes=[
            vmem((chunks, GRID, LANES), F32),
            vmem((halves, shots, rcv, LANES), BF16),
            vmem(code.shape, code.dtype),
            vmem((owned, rcv, samples), BF16),
            *[vmem(row.shape, row.dtype) for row in rows],
            vmem((owned, n_shot * ROWS, shots), BF16),
            vmem((owned, n_shot * ROWS, shots * ROWS), BF16),
            vmem((pieces, n_shot, part, LANES), F32),
            vmem((pieces, n_shot - 1, part, LANES), BF16),
            vmem((pieces, n_shot - 1, part, LANES), BF16),
            vmem((chunks, n_rcv - 1, CAP, LANES), BF16),
            vmem((chunks, n_rcv, CAP, LANES), BF16),
            vmem((slots, rcv), BF16),
            vmem((GRID, slots), BF16),
            dma((5 + halves * CUTS,)),
            dma((sems,)),
            dma((sems,)),
            dma((chunks, n_rcv - 1)),
            dma((chunks, n_rcv - 1)),
            dma((chunks,)),
        ],
        compiler_params=pltpu.CompilerParams(
            collective_id=0, has_side_effects=True, vmem_limit_bytes=56 * 2**20),
    )(shot_data, code, observed, *rows)


def solution(mesh):
    placed = (P("shot", "rcv", None), P(None, "shot"), P("shot", "rcv", None), P(), P(), P())
    body = functools.partial(on_device, mesh.shape["shot"], mesh.shape["rcv"])
    return jax.shard_map(
        body, mesh=mesh, in_specs=placed, out_specs=P("shot", "rcv", None), check_vma=False
    )
```

profile of v0, /device:TPU:0, one launch (start us, length us, event | category | flops | bytes accessed | tf_op | source)
XLA Modules:
  0.0 61.3 jit_solution(12141898017109187876)
XLA Ops:
  0.0 59.0 %shard_map.64 = f32[4,256,256]{2,1,0:T(8,128)} custom-call(bf16[32,256,256]{2,1,0:T(8,128)(2,1)} %shot_hbm.1, s32[32,32]{1,0:T(8,128)} %code_hbm.1, bf16[4,256,256]{2,1,0:T(8,128)(2,1)} %obs_hbm.1, s32[1,1024]{1,0:T(1,128)} %bitcast.5, s32[4,1024]{1,0:T(4,128)} %bitcast.3, f32[4,1024]{1,0:T(4,128)} %bitcast.4), custom_call_target="tpu_custom_call" | custom-call | tf_op jit(solution)/shard_map/pallas_call | solution.py:286
  59.0 2.3 %copy.8 = f32[4,256,256]{2,1,0:T(8,128)} copy(f32[4,256,256]{2,1,0:T(8,128)} %shard_map.64) | data formatting | bytes 2097152
where the time goes:
time: 61.5 us; the launch traced here: 61.3 us
  Pallas kernels  59 us (96%)
  local copies, waits for them, and re-layouts  2.29 us (4%)
    pallas_call x1, Pallas kernels, on_device(): pl.pallas_call(functools.partial(kernel, (n_shot, n_rcv, owned, halves),...  59 us
    unnamed x1, local copies, waits for them, and re-layouts  2.29 us

commit v1 on v0

--- a/solution.py
+++ b/solution.py
@@ -64,9 +64,9 @@
     return sorted(tasks)
 
 
-def kernel(dims, table, shot_hbm, code_hbm, obs_hbm, blk_hbm, idx_hbm, wgt_hbm, out_hbm,
-           out, shot, code_ref, obs, blk_ref, idx_ref, wgt_ref, signs, weights, acc, send, recv,
-           send3, recv3, select, slotm, load_sem, ssem, rsem, s3, r3, out_sem):
+def kernel(dims, table, shot_hbm, code_hbm, obs_hbm, blk_hbm, idx_hbm, wgt_hbm, out,
+           shot, code_ref, obs, blk_ref, idx_ref, wgt_ref, signs, weights, acc, send, recv,
+           send3, recv3, select, slotm, load_sem, ssem, rsem, s3, r3):
     n, groups, owned, halves = dims
     bits = n.bit_length() - 1
     shots, rcv, _ = shot_hbm.shape
@@ -207,16 +207,12 @@
             copy3(c, e).start()
         recv3[c, 0] = picked[:CAP]
 
-    def result(c):
-        j, h = c // halves, c % halves
-        return pltpu.make_async_copy(out.at[c], out_hbm.at[j, :, cut(h)], out_sem.at[c])
-
     def inject(c, _):
         for e in range(1, groups):
             copy3(c, e).wait_recv()
         arrived = recv3[c].reshape(slots, LANES)
-        out[c] = jnp.dot(slotm[...], arrived, preferred_element_type=F32)
-        result(c).start()
+        j, h = c // halves, c % halves
+        out[j, :, cut(h)] = jnp.dot(slotm[...], arrived, preferred_element_type=F32)
 
     def prepare():
         before = (lax.broadcasted_iota(jnp.int32, (rcv, rcv), 0)
@@ -267,7 +263,6 @@
     for c in range(chunks):
         for e in range(1, groups):
             copy3(c, e).wait_send()
-        result(c).wait()
 
 
 def on_device(n_shot, n_rcv, shot_data, code, observed, block_of, stencil_index, stencil_weight):
@@ -285,11 +280,10 @@
     rows = (block_of.T, stencil_index.T, stencil_weight.T)
     return pl.pallas_call(
         functools.partial(kernel, (n_shot, n_rcv, owned, halves), table),
-        out_shape=jax.ShapeDtypeStruct((owned, GRID, samples), F32),
+        out_shape=pltpu.VMEM((owned, GRID, samples), F32),
         in_specs=[hbm] * 6,
-        out_specs=hbm,
+        out_specs=pl.BlockSpec(memory_space=vmem),
         scratch_shapes=[
-            vmem((chunks, GRID, LANES), F32),
             vmem((halves, shots, rcv, LANES), BF16),
             vmem(code.shape, code.dtype),
             vmem((owned, rcv, samples), BF16),
@@ -308,11 +302,11 @@
             dma((sems,)),
             dma((chunks, n_rcv - 1)),
             dma((chunks, n_rcv - 1)),
-            dma((chunks,)),
         ],
         compiler_params=pltpu.CompilerParams(
-            collective_id=0, has_side_effects=True, vmem_limit_bytes=56 * 2**20),
-    )(shot_data, code, observed, *rows)
+            collective_id=0, has_side_effects=True, vmem_limit_bytes=40 * 2**20),
+    )(*[pltpu.with_memory_space_constraint(x, pltpu.HBM)
+        for x in (shot_data, code, observed, *rows)])
 
 
 def solution(mesh):

time: 61.5 us -> 59.6 us (0.969)
  local copies, waits for them, and re-layouts: 2.29 us -> 0.97 us
    unnamed x1, local copies, waits for them, and re-layouts: 2.29 us -> 0.97 us
    pallas_call x1, Pallas kernels: 59 us -> 58.4 us  [on_device(): pl.pallas_call(functools.partial(kernel, (n_shot, n_rcv, owned, halves),...]
where the time goes in v1:
time: 59.6 us; the launch traced here: 59.4 us
  Pallas kernels  58.4 us (98%)
  local copies, waits for them, and re-layouts  0.97 us (2%)
    pallas_call x1, Pallas kernels, on_device(): pl.pallas_call(functools.partial(kernel, (n_shot, n_rcv, owned, halves),...  58.4 us

profile of v1, /device:TPU:0, one launch (start us, length us, event | category | flops | bytes accessed | tf_op | source)
XLA Modules:
  0.0 59.4 jit_solution(11899827477061987569)
XLA Ops:
  0.0 58.4 %shard_map.64 = f32[4,256,256]{2,1,0:T(8,128)S(1)} custom-call(bf16[32,256,256]{2,1,0:T(8,128)(2,1)} %shot_hbm.1, s32[32,32]{1,0:T(8,128)} %code_hbm.1, bf16[4,256,256]{2,1,0:T(8,128)(2,1)} %obs_hbm.1, s32[1,1024]{1,0:T(1,128)} %bitcast.5, s32[4,1024]{1,0:T(4,128)} %bitcast.3, f32[4,1024]{1,0:T(4,128)} %bitcast.4), custom_call_target="tpu_custom_call" | custom-call | tf_op jit(solution)/shard_map/pallas_call | solution.py:281
  58.4 1.0 %copy.8 = f32[4,256,256]{2,1,0:T(8,128)} copy(f32[4,256,256]{2,1,0:T(8,128)S(1)} %shard_map.64) | data formatting | bytes 2097152

commit v2 on v1

--- a/solution.py
+++ b/solution.py
@@ -11,25 +11,29 @@
 CAP = 64
 ROWS = 16
 LANES = 128
-CUTS = 2
-AHEAD = 2
-LAG = 2.5
-LOW_FIRST = (1, 4, 7, 10)
-DIRECT = 2
+CUTS = 4
+AHEAD = 4
+LAG = 4
+HOLD = 3
+DIRECT = 5
+LOW_FIRST = 5 / 32
+LOW_SPAN = 20 / 32
 
 BF16, F32 = jnp.bfloat16, jnp.float32
 MESH = pl.DeviceIdType.MESH
 
 
 def stages_of(piece, pieces, bits):
-    rest = [(bit,) for bit in range(2, bits)]
+    rest = [(bit,) for bit in range(1, bits)]
+    low = max(1, round(pieces * LOW_FIRST))
+    span = round(pieces * LOW_SPAN)
     if bits == 1:
         return [(0,)]
     if piece >= pieces - DIRECT:
         return [(0,), tuple(range(1, bits))]
-    if piece in LOW_FIRST:
-        return [(1,), (0,)] + rest
-    return [(0,), (1,)] + rest
+    if piece in [1 + i * (span - 1) // low for i in range(low)]:
+        return rest + [(0,)]
+    return [(0,)] + rest
 
 
 def plan(pieces, bits):
@@ -39,28 +43,33 @@
         for group in stages_of(piece, pieces, bits):
             mask = sum(1 << bit for bit in group)
             kept = [m for m in left if not m & mask]
-            peers = []
+            first, peers = slot, []
             for peer in range(1, 1 << bits):
-                if peer & ~mask:
-                    continue
-                peers.append((peer, slot, sems))
-                slot, sems = slot + len(kept), sems + 1
-            stages.append((kept, peers))
-            left = kept
+                if not peer & ~mask:
+                    peers.append((peer, slot))
+                    slot += len(kept)
+            stages.append((kept, peers, (first, slot - first), sems))
+            left, sems = kept, sems + 1
         table.append(stages)
     return table, sems
 
 
 def schedule(table, halves_of):
-    tasks = []
+    hold, tasks, done = len(table) - HOLD, [], []
     for p, stages in enumerate(table):
+        late = stages[0][1][0][0] != 1
         tasks.append((max(p - AHEAD, -1), 0, p, "encode", 0))
         for s in range(len(stages) - 1):
-            tasks.append((p + LAG * s, 1, p, "sum", s))
+            at = p + LAG * s
+            if late and s == len(stages) - 2:
+                at = max(at, hold)
+            tasks.append((at, 1, p, "sum", s))
+        at = p + LAG * (len(stages) - 1)
+        done.append(max(at, hold + LAG) if late else at)
     for c, members in enumerate(halves_of):
-        done = max(p + LAG * (len(table[p]) - 1) for p in members)
-        tasks.append((done, 2, c, "finish", 0))
-        tasks.append((done + LAG, 3, c, "inject", 0))
+        at = max(done[p] for p in members)
+        tasks.append((at, 2, c, "finish", 0))
+        tasks.append((at + LAG, 3, c, "inject", 0))
     return sorted(tasks)
 
 
@@ -109,7 +118,8 @@
         load.start()
 
     barrier = pltpu.get_barrier_semaphore()
-    for mask in range(1, n):
+    near = [1 << bit for bit in range(bits)]
+    for mask in near:
         pl.semaphore_signal(barrier, inc=1, device_id={"shot": partners[mask]}, device_id_type=MESH)
     for e in range(1, groups):
         pl.semaphore_signal(barrier, inc=1, device_id={"rcv": rcv_peer(e)}, device_id_type=MESH)
@@ -128,18 +138,30 @@
         wide = jnp.dot(signs[j], spread_s, preferred_element_type=F32)
         weights[j] = jnp.where(same_row, wide, 0.0).astype(BF16)
 
+    def copy_of(p, slot, count, sem, peer):
+        c, some = p // CUTS, pl.ds(p % CUTS * part, part)
+        return pltpu.make_async_remote_copy(
+            src_ref=send.at[c, pl.ds(slot, count), some], dst_ref=recv.at[c, pl.ds(slot, count), some],
+            send_sem=ssem, recv_sem=rsem.at[sem],
+            device_id={"shot": partners[peer]}, device_id_type=MESH)
+
     def copies(p, s):
-        kept, peers = table[p][s]
-        return [pltpu.make_async_remote_copy(
-            src_ref=send.at[p, pl.ds(slot, len(kept))], dst_ref=recv.at[p, pl.ds(slot, len(kept))],
-            send_sem=ssem.at[sem], recv_sem=rsem.at[sem],
-            device_id={"shot": partners[peer]}, device_id_type=MESH)
-            for peer, slot, sem in peers]
+        kept, peers, _, sem = table[p][s]
+        return [copy_of(p, slot, len(kept), sem, peer) for peer, slot in peers]
+
+    def wait_for(p, s):
+        _, peers, (first, count), sem = table[p][s]
+        copy_of(p, first, count, sem, peers[0][0]).wait_recv()
 
     def copy3(c, e):
         return pltpu.make_async_remote_copy(
-            src_ref=send3.at[c, e - 1], dst_ref=recv3.at[c, e], send_sem=s3.at[c, e - 1],
-            recv_sem=r3.at[c, e - 1], device_id={"rcv": rcv_peer(e)}, device_id_type=MESH)
+            src_ref=send3.at[c, e - 1], dst_ref=recv3.at[c, e], send_sem=s3,
+            recv_sem=r3.at[c], device_id={"rcv": rcv_peer(e)}, device_id_type=MESH)
+
+    def copies3(c):
+        return pltpu.make_async_remote_copy(
+            src_ref=send3.at[c], dst_ref=recv3.at[c, pl.ds(1, groups - 1)], send_sem=s3,
+            recv_sem=r3.at[c], device_id={"rcv": rcv_peer(1)}, device_id_type=MESH)
 
     def place(p):
         return p // (halves * CUTS), p // CUTS % halves, p % CUTS
@@ -152,51 +174,52 @@
             widen(j)
         if j == 0:
             loads[h, q].wait()
-        kept, peers = table[p][0]
+        kept, peers, _, _ = table[p][0]
+        c = p // CUTS
 
         def tile(g, carry):
-            rows = pl.ds(pl.multiple_of(g * ROWS, ROWS), ROWS)
-            x = shot[h, :, pl.ds(pl.multiple_of(q * part + g * ROWS, ROWS), ROWS), :]
+            rows = pl.ds(pl.multiple_of(q * part + g * ROWS, ROWS), ROWS)
+            x = shot[h, :, rows, :]
             y = jnp.dot(weights[j], x.reshape(depth, LANES), preferred_element_type=F32)
             y = y.reshape(n, ROWS, LANES)
             for m in kept:
-                acc[p, m, rows, :] = y[m]
-            for peer, slot, _ in peers:
+                acc[c, m, rows, :] = y[m]
+            for peer, slot in peers:
                 for i, m in enumerate(kept):
-                    send[p, slot + i, rows, :] = y[m | peer].astype(BF16)
+                    send[c, slot + i, rows, :] = y[m | peer].astype(BF16)
             return carry
 
         lax.fori_loop(0, part // ROWS, tile, 0, unroll=4)
         if p == 0:
-            pl.semaphore_wait(barrier, n + groups - 2)
+            pl.semaphore_wait(barrier, len(near) + groups - 1)
         for copy in copies(p, 0):
             copy.start()
 
     def received(p, s, m):
-        kept, peers = table[p][s]
-        total = acc[p, m]
-        for _, slot, _ in peers:
-            total = total + recv[p, slot + kept.index(m)].astype(F32)
+        kept, peers, _, _ = table[p][s]
+        c, some = p // CUTS, pl.ds(p % CUTS * part, part)
+        total = acc[c, m, some]
+        for _, slot in peers:
+            total = total + recv[c, slot + kept.index(m), some].astype(F32)
         return total
 
     def sum_up(p, s):
-        for copy in copies(p, s):
-            copy.wait_recv()
-        kept, peers = table[p][s + 1]
-        for (peer, slot, _), copy in zip(peers, copies(p, s + 1)):
+        wait_for(p, s)
+        kept, peers, _, _ = table[p][s + 1]
+        c, some = p // CUTS, pl.ds(p % CUTS * part, part)
+        for (peer, slot), copy in zip(peers, copies(p, s + 1)):
             for i, m in enumerate(kept):
-                send[p, slot + i] = received(p, s, m | peer).astype(BF16)
+                send[c, slot + i, some] = received(p, s, m | peer).astype(BF16)
             copy.start()
         for m in kept:
-            acc[p, m] = received(p, s, m)
+            acc[c, m, some] = received(p, s, m)
 
     def finish(c, _):
         j, h = c // halves, c % halves
         picked = jnp.zeros((slots, LANES), F32)
         for q in range(CUTS):
             p = c * CUTS + q
-            for copy in copies(p, len(table[p]) - 1):
-                copy.wait_recv()
+            wait_for(p, len(table[p]) - 1)
             some = pl.ds(q * part, part)
             residual = received(p, len(table[p]) - 1, 0) - obs[j, some, cut(h)].astype(F32)
             picked = picked + jnp.dot(
@@ -208,8 +231,7 @@
         recv3[c, 0] = picked[:CAP]
 
     def inject(c, _):
-        for e in range(1, groups):
-            copy3(c, e).wait_recv()
+        copies3(c).wait_recv()
         arrived = recv3[c].reshape(slots, LANES)
         j, h = c // halves, c % halves
         out[j, :, cut(h)] = jnp.dot(slotm[...], arrived, preferred_element_type=F32)
@@ -256,13 +278,12 @@
             prepare()
             prepared = True
         act[what](item, s)
-    for p in range(len(table)):
-        for s in range(len(table[p])):
-            for copy in copies(p, s):
-                copy.wait_send()
-    for c in range(chunks):
-        for e in range(1, groups):
-            copy3(c, e).wait_send()
+    pltpu.make_async_remote_copy(
+        src_ref=send, dst_ref=recv, send_sem=ssem, recv_sem=rsem.at[0],
+        device_id={"shot": partners[1]}, device_id_type=MESH).wait_send()
+    pltpu.make_async_remote_copy(
+        src_ref=send3, dst_ref=send3, send_sem=s3, recv_sem=r3.at[0],
+        device_id={"rcv": rcv_peer(1)}, device_id_type=MESH).wait_send()
 
 
 def on_device(n_shot, n_rcv, shot_data, code, observed, block_of, stencil_index, stencil_weight):
@@ -271,7 +292,6 @@
     halves = samples // LANES
     chunks = owned * halves
     pieces = chunks * CUTS
-    part = rcv // CUTS
     slots = n_rcv * CAP
     table, sems = plan(pieces, n_shot.bit_length() - 1)
     hbm = pl.BlockSpec(memory_space=pltpu.HBM)
@@ -290,18 +310,18 @@
             *[vmem(row.shape, row.dtype) for row in rows],
             vmem((owned, n_shot * ROWS, shots), BF16),
             vmem((owned, n_shot * ROWS, shots * ROWS), BF16),
-            vmem((pieces, n_shot, part, LANES), F32),
-            vmem((pieces, n_shot - 1, part, LANES), BF16),
-            vmem((pieces, n_shot - 1, part, LANES), BF16),
+            vmem((chunks, n_shot, rcv, LANES), F32),
+            vmem((chunks, n_shot - 1, rcv, LANES), BF16),
+            vmem((chunks, n_shot - 1, rcv, LANES), BF16),
             vmem((chunks, n_rcv - 1, CAP, LANES), BF16),
             vmem((chunks, n_rcv, CAP, LANES), BF16),
             vmem((slots, rcv), BF16),
             vmem((GRID, slots), BF16),
             dma((5 + halves * CUTS,)),
+            dma,
             dma((sems,)),
-            dma((sems,)),
-            dma((chunks, n_rcv - 1)),
-            dma((chunks, n_rcv - 1)),
+            dma,
+            dma((chunks,)),
         ],
         compiler_params=pltpu.CompilerParams(
             collective_id=0, has_side_effects=True, vmem_limit_bytes=40 * 2**20),

time: 59.6 us -> 55.6 us (0.933)
  Pallas kernels: 58.4 us -> 54.4 us
    pallas_call x1, Pallas kernels: 58.4 us -> 54.4 us  [on_device(): pl.pallas_call(functools.partial(kernel, (n_shot, n_rcv, owned, halves),...]
where the time goes in v2:
time: 55.6 us; the launch traced here: 55.3 us
  Pallas kernels  54.4 us (98%)
  local copies, waits for them, and re-layouts  0.97 us (2%)
    pallas_call x1, Pallas kernels, on_device(): pl.pallas_call(functools.partial(kernel, (n_shot, n_rcv, owned, halves),...  54.4 us

profile of v2, /device:TPU:0, one launch (start us, length us, event | category | flops | bytes accessed | tf_op | source)
XLA Modules:
  0.0 55.3 jit_solution(15065252663356895072)
XLA Ops:
  0.0 54.4 %shard_map.64 = f32[4,256,256]{2,1,0:T(8,128)S(1)} custom-call(bf16[32,256,256]{2,1,0:T(8,128)(2,1)} %shot_hbm.1, s32[32,32]{1,0:T(8,128)} %code_hbm.1, bf16[4,256,256]{2,1,0:T(8,128)(2,1)} %obs_hbm.1, s32[1,1024]{1,0:T(1,128)} %bitcast.5, s32[4,1024]{1,0:T(4,128)} %bitcast.3, f32[4,1024]{1,0:T(4,128)} %bitcast.4), custom_call_target="tpu_custom_call" | custom-call | tf_op jit(solution)/shard_map/pallas_call | solution.py:301
  54.4 1.0 %copy.8 = f32[4,256,256]{2,1,0:T(8,128)} copy(f32[4,256,256]{2,1,0:T(8,128)S(1)} %shard_map.64) | data formatting | bytes 2097152

commit v3 on v2

--- a/solution.py
+++ b/solution.py
@@ -16,6 +16,7 @@
 LAG = 4
 HOLD = 3
 DIRECT = 5
+SPLIT = 0
 LOW_FIRST = 5 / 32
 LOW_SPAN = 20 / 32
 
@@ -36,8 +37,17 @@
     return [(0,)] + rest
 
 
+def cut_up(chunks, rcv):
+    part = rcv // CUTS
+    pieces = [(c, q * part, part) for c in range(chunks) for q in range(CUTS)]
+    for _ in range(SPLIT if part % (2 * ROWS) == 0 else 0):
+        c, row, rows = pieces.pop()
+        pieces += [(c, row, rows // 2), (c, row + rows // 2, rows // 2)]
+    return pieces
+
+
 def plan(pieces, bits):
-    table, sems = [], 0
+    table = []
     for piece in range(pieces):
         left, slot, stages = list(range(1 << bits)), 0, []
         for group in stages_of(piece, pieces, bits):
@@ -48,10 +58,10 @@
                 if not peer & ~mask:
                     peers.append((peer, slot))
                     slot += len(kept)
-            stages.append((kept, peers, (first, slot - first), sems))
-            left, sems = kept, sems + 1
+            stages.append((kept, peers, (first, slot - first)))
+            left = kept
         table.append(stages)
-    return table, sems
+    return table
 
 
 def schedule(table, halves_of):
@@ -73,13 +83,44 @@
     return sorted(tasks)
 
 
-def kernel(dims, table, shot_hbm, code_hbm, obs_hbm, blk_hbm, idx_hbm, wgt_hbm, out,
+def members_of(pieces):
+    last = pieces[-1][0]
+    return [[p for p, piece in enumerate(pieces) if piece[0] == c] for c in range(last + 1)]
+
+
+def share_out(table, tasks, members):
+    sent, waited, taken = {}, {}, {}
+    for at, (_, _, item, what, s) in enumerate(tasks):
+        if what == "encode":
+            sent[item, 0] = at
+        elif what == "sum":
+            sent[item, s + 1] = at
+            waited[item, s] = at
+        elif what == "finish":
+            for p in members[item]:
+                waited[p, len(table[p]) - 1] = at
+    group = {key: tuple(peer for peer, _ in table[key[0]][key[1]][1]) for key in sent}
+    last, sem_of = [], {}
+    for key in sorted(sent, key=sent.get):
+        reply = [k for k in sent if group[k] == group[key] and waited[k] <= sent[key]]
+        for sem, old in enumerate(last):
+            if group[old] == group[key] and any(waited[old] <= sent[k] for k in reply):
+                sem_of[key], last[sem] = sem, key
+                break
+        else:
+            sem_of[key] = len(last)
+            last.append(key)
+    return sem_of, len(last)
+
+
+def kernel(dims, pieces, table, tasks, sem_of, shot_hbm, code_hbm, obs_hbm, blk_hbm, idx_hbm, wgt_hbm, out,
            shot, code_ref, obs, blk_ref, idx_ref, wgt_ref, signs, weights, acc, send, recv,
-           send3, recv3, select, slotm, load_sem, ssem, rsem, s3, r3):
+           send3, recv3, left, select, slotm, load_sem, ssem, rsem, s3, r3):
     n, groups, owned, halves = dims
     bits = n.bit_length() - 1
     shots, rcv, _ = shot_hbm.shape
     part = rcv // CUTS
+    members = members_of(pieces)
     chunks = owned * halves
     slots = groups * CAP
     me = lax.axis_index("shot")
@@ -139,19 +180,20 @@
         weights[j] = jnp.where(same_row, wide, 0.0).astype(BF16)
 
     def copy_of(p, slot, count, sem, peer):
-        c, some = p // CUTS, pl.ds(p % CUTS * part, part)
+        c, row, rows = pieces[p]
+        some = pl.ds(row, rows)
         return pltpu.make_async_remote_copy(
             src_ref=send.at[c, pl.ds(slot, count), some], dst_ref=recv.at[c, pl.ds(slot, count), some],
             send_sem=ssem, recv_sem=rsem.at[sem],
             device_id={"shot": partners[peer]}, device_id_type=MESH)
 
     def copies(p, s):
-        kept, peers, _, sem = table[p][s]
-        return [copy_of(p, slot, len(kept), sem, peer) for peer, slot in peers]
+        kept, peers, _ = table[p][s]
+        return [copy_of(p, slot, len(kept), sem_of[p, s], peer) for peer, slot in peers]
 
     def wait_for(p, s):
-        _, peers, (first, count), sem = table[p][s]
-        copy_of(p, first, count, sem, peers[0][0]).wait_recv()
+        _, peers, (first, count) = table[p][s]
+        copy_of(p, first, count, sem_of[p, s], peers[0][0]).wait_recv()
 
     def copy3(c, e):
         return pltpu.make_async_remote_copy(
@@ -163,22 +205,19 @@
             src_ref=send3.at[c], dst_ref=recv3.at[c, pl.ds(1, groups - 1)], send_sem=s3,
             recv_sem=r3.at[c], device_id={"rcv": rcv_peer(1)}, device_id_type=MESH)
 
-    def place(p):
-        return p // (halves * CUTS), p // CUTS % halves, p % CUTS
-
     def encode(p, _):
-        j, h, q = place(p)
-        if h == 0 and q == 0:
+        c, row, size = pieces[p]
+        j, h = c // halves, c % halves
+        if h == 0 and row == 0:
             if j == 0:
                 small[0].wait()
             widen(j)
         if j == 0:
-            loads[h, q].wait()
-        kept, peers, _, _ = table[p][0]
-        c = p // CUTS
+            loads[h, row // part].wait()
+        kept, peers, _ = table[p][0]
 
         def tile(g, carry):
-            rows = pl.ds(pl.multiple_of(q * part + g * ROWS, ROWS), ROWS)
+            rows = pl.ds(pl.multiple_of(row + g * ROWS, ROWS), ROWS)
             x = shot[h, :, rows, :]
             y = jnp.dot(weights[j], x.reshape(depth, LANES), preferred_element_type=F32)
             y = y.reshape(n, ROWS, LANES)
@@ -189,15 +228,16 @@
                     send[c, slot + i, rows, :] = y[m | peer].astype(BF16)
             return carry
 
-        lax.fori_loop(0, part // ROWS, tile, 0, unroll=4)
+        lax.fori_loop(0, size // ROWS, tile, 0, unroll=min(4, size // ROWS))
         if p == 0:
             pl.semaphore_wait(barrier, len(near) + groups - 1)
         for copy in copies(p, 0):
             copy.start()
 
     def received(p, s, m):
-        kept, peers, _, _ = table[p][s]
-        c, some = p // CUTS, pl.ds(p % CUTS * part, part)
+        kept, peers, _ = table[p][s]
+        c, row, rows = pieces[p]
+        some = pl.ds(row, rows)
         total = acc[c, m, some]
         for _, slot in peers:
             total = total + recv[c, slot + kept.index(m), some].astype(F32)
@@ -205,8 +245,9 @@
 
     def sum_up(p, s):
         wait_for(p, s)
-        kept, peers, _, _ = table[p][s + 1]
-        c, some = p // CUTS, pl.ds(p % CUTS * part, part)
+        kept, peers, _ = table[p][s + 1]
+        c, row, rows = pieces[p]
+        some = pl.ds(row, rows)
         for (peer, slot), copy in zip(peers, copies(p, s + 1)):
             for i, m in enumerate(kept):
                 send[c, slot + i, some] = received(p, s, m | peer).astype(BF16)
@@ -216,15 +257,13 @@
 
     def finish(c, _):
         j, h = c // halves, c % halves
-        picked = jnp.zeros((slots, LANES), F32)
-        for q in range(CUTS):
-            p = c * CUTS + q
+        for p in members[c]:
+            _, row, rows = pieces[p]
+            some = pl.ds(row, rows)
             wait_for(p, len(table[p]) - 1)
-            some = pl.ds(q * part, part)
             residual = received(p, len(table[p]) - 1, 0) - obs[j, some, cut(h)].astype(F32)
-            picked = picked + jnp.dot(
-                select[:, some], residual.astype(BF16), preferred_element_type=F32)
-        picked = picked.astype(BF16)
+            left[c, some] = residual.astype(BF16)
+        picked = jnp.dot(select[...], left[c], preferred_element_type=F32).astype(BF16)
         for e in range(1, groups):
             send3[c, e - 1] = picked[e * CAP:(e + 1) * CAP]
             copy3(c, e).start()
@@ -270,8 +309,7 @@
 
     act = {"encode": encode, "sum": sum_up, "finish": finish, "inject": inject}
     prepared = False
-    members = [[c * CUTS + q for q in range(CUTS)] for c in range(chunks)]
-    for _, _, item, what, s in schedule(table, members):
+    for _, _, item, what, s in tasks:
         if what != "encode" and not prepared:
             for load in small[1:]:
                 load.wait()
@@ -291,15 +329,18 @@
     owned = observed.shape[0]
     halves = samples // LANES
     chunks = owned * halves
-    pieces = chunks * CUTS
+    pieces = cut_up(chunks, rcv)
     slots = n_rcv * CAP
-    table, sems = plan(pieces, n_shot.bit_length() - 1)
+    table = plan(len(pieces), n_shot.bit_length() - 1)
+    members = members_of(pieces)
+    tasks = schedule(table, members)
+    sem_of, sems = share_out(table, tasks, members)
     hbm = pl.BlockSpec(memory_space=pltpu.HBM)
     vmem = pltpu.VMEM
     dma = pltpu.SemaphoreType.DMA
     rows = (block_of.T, stencil_index.T, stencil_weight.T)
     return pl.pallas_call(
-        functools.partial(kernel, (n_shot, n_rcv, owned, halves), table),
+        functools.partial(kernel, (n_shot, n_rcv, owned, halves), pieces, table, tasks, sem_of),
         out_shape=pltpu.VMEM((owned, GRID, samples), F32),
         in_specs=[hbm] * 6,
         out_specs=pl.BlockSpec(memory_space=vmem),
@@ -315,6 +356,7 @@
             vmem((chunks, n_shot - 1, rcv, LANES), BF16),
             vmem((chunks, n_rcv - 1, CAP, LANES), BF16),
             vmem((chunks, n_rcv, CAP, LANES), BF16),
+            vmem((chunks, rcv, LANES), BF16),
             vmem((slots, rcv), BF16),
             vmem((GRID, slots), BF16),
             dma((5 + halves * CUTS,)),

time: 55.6 us -> 55.2 us (level)
  no operation moved by 1% of the time
where the time goes in v3:
time: 55.2 us; the launch traced here: 55 us
  Pallas kernels  54 us (98%)
  local copies, waits for them, and re-layouts  0.97 us (2%)
    pallas_call x1, Pallas kernels, on_device(): pl.pallas_call(functools.partial(kernel, (n_shot, n_rcv, owned, halves),...  54 us

profile of v3, /device:TPU:0, one launch (start us, length us, event | category | flops | bytes accessed | tf_op | source)
XLA Modules:
  0.0 55.0 jit_solution(5287085984499071510)
XLA Ops:
  0.0 54.0 %shard_map.64 = f32[4,256,256]{2,1,0:T(8,128)S(1)} custom-call(bf16[32,256,256]{2,1,0:T(8,128)(2,1)} %shot_hbm.1, s32[32,32]{1,0:T(8,128)} %code_hbm.1, bf16[4,256,256]{2,1,0:T(8,128)(2,1)} %obs_hbm.1, s32[1,1024]{1,0:T(1,128)} %bitcast.5, s32[4,1024]{1,0:T(4,128)} %bitcast.3, f32[4,1024]{1,0:T(4,128)} %bitcast.4), custom_call_target="tpu_custom_call" | custom-call | tf_op jit(solution)/shard_map/pallas_call | solution.py:342
  54.0 1.0 %copy.8 = f32[4,256,256]{2,1,0:T(8,128)} copy(f32[4,256,256]{2,1,0:T(8,128)S(1)} %shard_map.64) | data formatting | bytes 2097152

commit v4 on v3

--- a/solution.py
+++ b/solution.py
@@ -15,8 +15,12 @@
 AHEAD = 4
 LAG = 4
 HOLD = 3
-DIRECT = 5
+DIRECT = 4
 SPLIT = 0
+EARLY = 2
+PICK_AT = 3
+PICK_STEP = 0.75
+INJECT_LAG = 2
 LOW_FIRST = 5 / 32
 LOW_SPAN = 20 / 32
 
@@ -64,8 +68,13 @@
     return table
 
 
-def schedule(table, halves_of):
+def schedule(table, halves_of, early):
     hold, tasks, done = len(table) - HOLD, [], []
+    plain = len(halves_of) - early
+    for i in range(early):
+        for s in range(CUTS + 3):
+            at = PICK_AT + PICK_STEP * (i * (CUTS + 3) + s)
+            tasks.append((at, 0, plain + i, "pick", s))
     for p, stages in enumerate(table):
         late = stages[0][1][0][0] != 1
         tasks.append((max(p - AHEAD, -1), 0, p, "encode", 0))
@@ -78,8 +87,9 @@
         done.append(max(at, hold + LAG) if late else at)
     for c, members in enumerate(halves_of):
         at = max(done[p] for p in members)
-        tasks.append((at, 2, c, "finish", 0))
-        tasks.append((at + LAG, 3, c, "inject", 0))
+        tasks.append((at, 2 if c < plain else 4, c, "finish", 0))
+        if c < plain:
+            tasks.append((at + INJECT_LAG, 3, c, "inject", 0))
     return sorted(tasks)
 
 
@@ -115,13 +125,14 @@
 
 def kernel(dims, pieces, table, tasks, sem_of, shot_hbm, code_hbm, obs_hbm, blk_hbm, idx_hbm, wgt_hbm, out,
            shot, code_ref, obs, blk_ref, idx_ref, wgt_ref, signs, weights, acc, send, recv,
-           send3, recv3, left, select, slotm, load_sem, ssem, rsem, s3, r3):
-    n, groups, owned, halves = dims
+           send3, recv3, left, full, sendx, recvx, select, slotm, load_sem, ssem, rsem, s3, r3, sx, rx):
+    n, groups, owned, halves, early = dims
     bits = n.bit_length() - 1
     shots, rcv, _ = shot_hbm.shape
     part = rcv // CUTS
     members = members_of(pieces)
     chunks = owned * halves
+    plain = chunks - early
     slots = groups * CAP
     me = lax.axis_index("shot")
     mine = lax.axis_index("rcv")
@@ -205,30 +216,77 @@
             src_ref=send3.at[c], dst_ref=recv3.at[c, pl.ds(1, groups - 1)], send_sem=s3,
             recv_sem=r3.at[c], device_id={"rcv": rcv_peer(1)}, device_id_type=MESH)
 
-    def encode(p, _):
-        c, row, size = pieces[p]
+    def copyx(i, e):
+        return pltpu.make_async_remote_copy(
+            src_ref=sendx.at[i, e - 1], dst_ref=recvx.at[i, e], send_sem=sx,
+            recv_sem=rx.at[i], device_id={"rcv": rcv_peer(e)}, device_id_type=MESH)
+
+    def copiesx(i):
+        return pltpu.make_async_remote_copy(
+            src_ref=sendx.at[i], dst_ref=recvx.at[i, pl.ds(1, groups - 1)], send_sem=sx,
+            recv_sem=rx.at[i], device_id={"rcv": rcv_peer(1)}, device_id_type=MESH)
+
+    widened = set()
+
+    def mix(c, row, size, put):
         j, h = c // halves, c % halves
-        if h == 0 and row == 0:
-            if j == 0:
+        if j not in widened:
+            if not widened:
                 small[0].wait()
+            widened.add(j)
             widen(j)
         if j == 0:
             loads[h, row // part].wait()
-        kept, peers, _ = table[p][0]
 
         def tile(g, carry):
             rows = pl.ds(pl.multiple_of(row + g * ROWS, ROWS), ROWS)
             x = shot[h, :, rows, :]
             y = jnp.dot(weights[j], x.reshape(depth, LANES), preferred_element_type=F32)
-            y = y.reshape(n, ROWS, LANES)
+            put(rows, y.reshape(n, ROWS, LANES))
+            return carry
+
+        lax.fori_loop(0, size // ROWS, tile, 0, unroll=min(4, size // ROWS))
+
+    def pick(c, s):
+        i, j, h = c - plain, c // halves, c % halves
+        if s < CUTS:
+            def put(rows, y):
+                full[:, rows, :] = y.astype(BF16)
+
+            mix(c, s * part, part, put)
+            return
+        third = -(-(n + 1) // 3)
+        for m in range((s - CUTS) * third, min(n + 1, (s - CUTS + 1) * third)):
+            rows = full[m] if m < n else obs[j, :, cut(h)]
+            picked = jnp.dot(select[...], rows, preferred_element_type=F32).astype(BF16)
+            recvx[i, 0, m] = picked[:CAP]
+            for e in range(1, groups):
+                sendx[i, e - 1, m] = picked[e * CAP:(e + 1) * CAP]
+        if s == CUTS + 2:
+            for e in range(1, groups):
+                copyx(i, e).start()
+
+    def encode(p, _):
+        c, row, size = pieces[p]
+        kept, peers, _ = table[p][0]
+        if c >= plain:
+            i, e, some = c - plain, row // CAP, pl.ds(row, size)
+            if row == 0:
+                copiesx(i).wait_recv()
             for m in kept:
-                acc[c, m, rows, :] = y[m]
+                acc[c, m, some] = recvx[i, e, m].astype(F32)
             for peer, slot in peers:
-                for i, m in enumerate(kept):
-                    send[c, slot + i, rows, :] = y[m | peer].astype(BF16)
-            return carry
-
-        lax.fori_loop(0, size // ROWS, tile, 0, unroll=min(4, size // ROWS))
+                for k, m in enumerate(kept):
+                    send[c, slot + k, some] = recvx[i, e, m | peer]
+        else:
+            def put(rows, y):
+                for m in kept:
+                    acc[c, m, rows, :] = y[m]
+                for peer, slot in peers:
+                    for i, m in enumerate(kept):
+                        send[c, slot + i, rows, :] = y[m | peer].astype(BF16)
+
+            mix(c, row, size, put)
         if p == 0:
             pl.semaphore_wait(barrier, len(near) + groups - 1)
         for copy in copies(p, 0):
@@ -261,8 +319,12 @@
             _, row, rows = pieces[p]
             some = pl.ds(row, rows)
             wait_for(p, len(table[p]) - 1)
-            residual = received(p, len(table[p]) - 1, 0) - obs[j, some, cut(h)].astype(F32)
+            seen = obs[j, some, cut(h)] if c < plain else recvx[c - plain, row // CAP, n]
+            residual = received(p, len(table[p]) - 1, 0) - seen.astype(F32)
             left[c, some] = residual.astype(BF16)
+        if c >= plain:
+            out[j, :, cut(h)] = jnp.dot(slotm[...], left[c], preferred_element_type=F32)
+            return
         picked = jnp.dot(select[...], left[c], preferred_element_type=F32).astype(BF16)
         for e in range(1, groups):
             send3[c, e - 1] = picked[e * CAP:(e + 1) * CAP]
@@ -307,7 +369,7 @@
                 spread.astype(BF16), pick, (((1,), (1,)), ((), ())), preferred_element_type=F32)
         slotm[...] = total.astype(BF16)
 
-    act = {"encode": encode, "sum": sum_up, "finish": finish, "inject": inject}
+    act = {"pick": pick, "encode": encode, "sum": sum_up, "finish": finish, "inject": inject}
     prepared = False
     for _, _, item, what, s in tasks:
         if what != "encode" and not prepared:
@@ -322,6 +384,10 @@
     pltpu.make_async_remote_copy(
         src_ref=send3, dst_ref=send3, send_sem=s3, recv_sem=r3.at[0],
         device_id={"rcv": rcv_peer(1)}, device_id_type=MESH).wait_send()
+    if early:
+        pltpu.make_async_remote_copy(
+            src_ref=sendx, dst_ref=sendx, send_sem=sx, recv_sem=rx.at[0],
+            device_id={"rcv": rcv_peer(1)}, device_id_type=MESH).wait_send()
 
 
 def on_device(n_shot, n_rcv, shot_data, code, observed, block_of, stencil_index, stencil_weight):
@@ -331,16 +397,20 @@
     chunks = owned * halves
     pieces = cut_up(chunks, rcv)
     slots = n_rcv * CAP
+    part = rcv // CUTS
     table = plan(len(pieces), n_shot.bit_length() - 1)
     members = members_of(pieces)
-    tasks = schedule(table, members)
+    early = EARLY if slots == rcv and part == CAP and SPLIT == 0 else 0
+    tasks = schedule(table, members, early)
+    kinds = max(early, 1)
+    plain = chunks - early
     sem_of, sems = share_out(table, tasks, members)
     hbm = pl.BlockSpec(memory_space=pltpu.HBM)
     vmem = pltpu.VMEM
     dma = pltpu.SemaphoreType.DMA
     rows = (block_of.T, stencil_index.T, stencil_weight.T)
     return pl.pallas_call(
-        functools.partial(kernel, (n_shot, n_rcv, owned, halves), pieces, table, tasks, sem_of),
+        functools.partial(kernel, (n_shot, n_rcv, owned, halves, early), pieces, table, tasks, sem_of),
         out_shape=pltpu.VMEM((owned, GRID, samples), F32),
         in_specs=[hbm] * 6,
         out_specs=pl.BlockSpec(memory_space=vmem),
@@ -354,16 +424,21 @@
             vmem((chunks, n_shot, rcv, LANES), F32),
             vmem((chunks, n_shot - 1, rcv, LANES), BF16),
             vmem((chunks, n_shot - 1, rcv, LANES), BF16),
-            vmem((chunks, n_rcv - 1, CAP, LANES), BF16),
-            vmem((chunks, n_rcv, CAP, LANES), BF16),
+            vmem((plain, n_rcv - 1, CAP, LANES), BF16),
+            vmem((plain, n_rcv, CAP, LANES), BF16),
             vmem((chunks, rcv, LANES), BF16),
+            vmem((n_shot, rcv, LANES), BF16),
+            vmem((kinds, n_rcv - 1, n_shot + 1, CAP, LANES), BF16),
+            vmem((kinds, n_rcv, n_shot + 1, CAP, LANES), BF16),
             vmem((slots, rcv), BF16),
             vmem((GRID, slots), BF16),
             dma((5 + halves * CUTS,)),
             dma,
             dma((sems,)),
             dma,
-            dma((chunks,)),
+            dma((plain,)),
+            dma,
+            dma((kinds,)),
         ],
         compiler_params=pltpu.CompilerParams(
             collective_id=0, has_side_effects=True, vmem_limit_bytes=40 * 2**20),

time: 55.2 us -> 52.8 us (0.957)
  Pallas kernels: 54 us -> 51.6 us
    pallas_call x1, Pallas kernels: 54 us -> 51.6 us  [on_device(): pl.pallas_call(functools.partial(kernel, (n_shot, n_rcv, owned, halves, e...]
where the time goes in v4:
time: 52.8 us; the launch traced here: 52.6 us
  Pallas kernels  51.6 us (98%)
  local copies, waits for them, and re-layouts  0.97 us (2%)
    pallas_call x1, Pallas kernels, on_device(): pl.pallas_call(functools.partial(kernel, (n_shot, n_rcv, owned, halves, e...  51.6 us

profile of v4, /device:TPU:0, one launch (start us, length us, event | category | flops | bytes accessed | tf_op | source)
XLA Modules:
  0.0 52.6 jit_solution(15930735045380407655)
XLA Ops:
  0.0 51.6 %shard_map.64 = f32[4,256,256]{2,1,0:T(8,128)S(1)} custom-call(bf16[32,256,256]{2,1,0:T(8,128)(2,1)} %shot_hbm.1, s32[32,32]{1,0:T(8,128)} %code_hbm.1, bf16[4,256,256]{2,1,0:T(8,128)(2,1)} %obs_hbm.1, s32[1,1024]{1,0:T(1,128)} %bitcast.5, s32[4,1024]{1,0:T(4,128)} %bitcast.3, f32[4,1024]{1,0:T(4,128)} %bitcast.4), custom_call_target="tpu_custom_call" | custom-call | tf_op jit(solution)/shard_map/pallas_call | solution.py:412
  51.6 1.0 %copy.8 = f32[4,256,256]{2,1,0:T(8,128)} copy(f32[4,256,256]{2,1,0:T(8,128)S(1)} %shard_map.64) | data formatting | bytes 2097152

commit v5 on v4

--- a/solution.py
+++ b/solution.py
@@ -21,6 +21,8 @@
 PICK_AT = 3
 PICK_STEP = 0.75
 INJECT_LAG = 2
+SOONER = 0.5
+LATER = 0.25
 LOW_FIRST = 5 / 32
 LOW_SPAN = 20 / 32
 
@@ -87,9 +89,13 @@
         done.append(max(at, hold + LAG) if late else at)
     for c, members in enumerate(halves_of):
         at = max(done[p] for p in members)
-        tasks.append((at, 2 if c < plain else 4, c, "finish", 0))
         if c < plain:
-            tasks.append((at + INJECT_LAG, 3, c, "inject", 0))
+            at -= SOONER if at < hold + LAG else 0
+            tasks.append((at, 2, c, "finish", 0))
+            inject = max(at + INJECT_LAG, hold + LAG + 0.5)
+            tasks.append((inject + 0.1 * c, 3, c, "inject", 0))
+        else:
+            tasks.append((at + LATER, 4, c, "finish", 0))
     return sorted(tasks)
 
 

time: 52.8 us -> 52.8 us (level)
  no operation moved by 1% of the time
where the time goes in v5:
time: 52.8 us; the launch traced here: 52.6 us
  Pallas kernels  51.6 us (98%)
  local copies, waits for them, and re-layouts  0.97 us (2%)
    pallas_call x1, Pallas kernels, on_device(): pl.pallas_call(functools.partial(kernel, (n_shot, n_rcv, owned, halves, e...  51.6 us

profile of v5, /device:TPU:0, one launch (start us, length us, event | category | flops | bytes accessed | tf_op | source)
XLA Modules:
  0.0 52.6 jit_solution(8219747616177839649)
XLA Ops:
  0.0 51.6 %shard_map.64 = f32[4,256,256]{2,1,0:T(8,128)S(1)} custom-call(bf16[32,256,256]{2,1,0:T(8,128)(2,1)} %shot_hbm.1, s32[32,32]{1,0:T(8,128)} %code_hbm.1, bf16[4,256,256]{2,1,0:T(8,128)(2,1)} %obs_hbm.1, s32[1,1024]{1,0:T(1,128)} %bitcast.5, s32[4,1024]{1,0:T(4,128)} %bitcast.3, f32[4,1024]{1,0:T(4,128)} %bitcast.4), custom_call_target="tpu_custom_call" | custom-call | tf_op jit(solution)/shard_map/pallas_call | solution.py:418
  51.6 1.0 %copy.8 = f32[4,256,256]{2,1,0:T(8,128)} copy(f32[4,256,256]{2,1,0:T(8,128)S(1)} %shard_map.64) | data formatting | bytes 2097152

commit v6 on v5

--- a/solution.py
+++ b/solution.py
@@ -14,10 +14,10 @@
 CUTS = 4
 AHEAD = 4
 LAG = 4
-HOLD = 3
+HOLD = 4
 DIRECT = 4
 SPLIT = 0
-EARLY = 2
+EARLY = 3
 PICK_AT = 3
 PICK_STEP = 0.75
 INJECT_LAG = 2

time: 52.8 us -> 52.7 us (level)
  no operation moved by 1% of the time
where the time goes in v6:
time: 52.7 us; the launch traced here: 52.5 us
  Pallas kernels  51.5 us (98%)
  local copies, waits for them, and re-layouts  0.97 us (2%)
    pallas_call x1, Pallas kernels, on_device(): pl.pallas_call(functools.partial(kernel, (n_shot, n_rcv, owned, halves, e...  51.5 us

profile of v6, /device:TPU:0, one launch (start us, length us, event | category | flops | bytes accessed | tf_op | source)
XLA Modules:
  0.0 52.5 jit_solution(14885128723476522502)
XLA Ops:
  0.0 51.5 %shard_map.64 = f32[4,256,256]{2,1,0:T(8,128)S(1)} custom-call(bf16[32,256,256]{2,1,0:T(8,128)(2,1)} %shot_hbm.1, s32[32,32]{1,0:T(8,128)} %code_hbm.1, bf16[4,256,256]{2,1,0:T(8,128)(2,1)} %obs_hbm.1, s32[1,1024]{1,0:T(1,128)} %bitcast.5, s32[4,1024]{1,0:T(4,128)} %bitcast.3, f32[4,1024]{1,0:T(4,128)} %bitcast.4), custom_call_target="tpu_custom_call" | custom-call | tf_op jit(solution)/shard_map/pallas_call | solution.py:418
  51.6 1.0 %copy.8 = f32[4,256,256]{2,1,0:T(8,128)} copy(f32[4,256,256]{2,1,0:T(8,128)S(1)} %shard_map.64) | data formatting | bytes 2097152
